TPU v7x, 32 devices: a whole 2x2x4 slice. The times are simulated.
32 devices in a mesh: batch: 4 (over y, x), centre: 8 (over z, core).
Axes of the slice: x: 2, y: 2, z: 4, core: 2. Of those that a mesh axis runs over, the one named last changes fastest.
Arguments:
- pool: float32 [1024, 1024], P('batch', 'centre'), may hold values from -4.5 to 4.5
- sample_index: int32 [512], P('batch'), may hold values from 0 to 255
- targets: float32 [512, 256], P('batch'), may hold values from -6 to 6
- centres: float32 [512, 1024], P(('batch', 'centre')), may hold values from -4.5 to 4.5
- coeffs: float32 [512, 256], P(('batch', 'centre')), may hold values from -6 to 6
- eigvecs: float32 [512, 1024], P(('batch', 'centre')), may hold values from -0.75 to 0.75
- eigscale: float32 [1024], replicated, may hold values from 0.1 to 0.95
Outputs:
- new_coeffs: float32 [512, 256], P(('batch', 'centre'))
Inputs may be any that keep to these rules, and one draw needn't show every extreme that they name: `sample_index`: each batch row's sample lies in the block of 256 training samples held by its own batch group; the index counts within that block.
All inputs are finite; a program needn't handle non-finite values.
Results may differ from a plain program's by a relative error of at most 0.0003.
Values sent between devices are 32-bit elements; how exact they have to be, the bound alone decides.
A program may use at most 64 MiB of HBM per device.

v0:
```python
import jax
import jax.numpy as jnp
from jax import lax
from jax.sharding import PartitionSpec as P


def on_device(pool, sample_index, targets, centres, coeffs, eigvecs, eigscale):
    highest = lax.Precision.HIGHEST
    picked = jnp.take(pool, sample_index, axis=0)
    batch_x = lax.all_gather(picked, "centre", axis=1, tiled=True)
    row_count = batch_x.shape[0]
    n_batch = lax.axis_size("batch")
    n_centre = lax.axis_size("centre")
    own_centres = centres.shape[0]
    group_rows = own_centres * n_batch
    total_centres = group_rows * n_centre
    total_rows = row_count * n_batch
    width = batch_x.shape[1]
    inv_width = 1.0 / jnp.sqrt(jnp.float32(width))
    model_norm = 1.0 / jnp.sqrt(jnp.float32(total_centres))
    zrows = lax.all_gather(centres, "batch", axis=0, tiled=True)
    crows = lax.all_gather(coeffs, "batch", axis=0, tiled=True)
    scores = lax.dot_general(
        batch_x,
        zrows,
        (((1,), (1,)), ((), ())),
        precision=highest,
        preferred_element_type=jnp.float32,
    )
    kpiece = jnp.exp(scores * inv_width)
    partial_value = jnp.dot(kpiece, crows, precision=highest, preferred_element_type=jnp.float32)
    kernel, partial_value = (kpiece, partial_value)
    columns = (
        lax.psum_scatter(partial_value, "centre", scatter_dimension=1, tiled=True) * model_norm
    )
    col_width = columns.shape[1]
    col_offset = lax.axis_index("centre") * col_width
    own_targets = lax.dynamic_slice_in_dim(targets, col_offset, col_width, 1)
    residual = lax.all_gather(columns - own_targets, "centre", axis=1, tiled=True)
    gradient = (
        lax.psum_scatter(
            lax.dot_general(
                kernel,
                residual,
                (((0,), (0,)), ((), ())),
                precision=highest,
                preferred_element_type=jnp.float32,
            ),
            "batch",
            scatter_dimension=0,
            tiled=True,
        )
        * model_norm
    )
    local_coords = lax.dot_general(
        eigvecs,
        gradient,
        (((0,), (0,)), ((), ())),
        precision=highest,
        preferred_element_type=jnp.float32,
    )
    coords = lax.psum(local_coords, ("batch", "centre"))
    correction = jnp.dot(
        eigvecs, eigscale[:, None] * coords, precision=highest, preferred_element_type=jnp.float32
    )
    step_size = 0.5 * jnp.sqrt(jnp.float32(total_centres) / jnp.float32(total_rows))
    return coeffs - step_size * (gradient - correction)


def solution(mesh):
    return jax.shard_map(
        on_device,
        mesh=mesh,
        in_specs=(
            P("batch", "centre"),
            P("batch"),
            P("batch", None),
            P(("batch", "centre"), None),
            P(("batch", "centre"), None),
            P(("batch", "centre"), None),
            P(),
        ),
        out_specs=P(("batch", "centre"), None),
        check_vma=False,
    )
```

profile of v0, /device:TPU:0, one launch (start us, length us, event | category | flops | bytes accessed | tf_op | source)
XLA Modules:
  0.0 257.5 jit_solution(9517945055729336617)
XLA Ops:
  6.5 0.0 copy-start
  6.5 0.0 copy-start.7
  6.5 0.0 copy-start.4
  6.5 0.0 reduce-scatter.7.cloned.1.call-start
  6.5 0.7 compare_and_fusion
  7.3 0.0 copy-done.7
  7.3 9.9 %all_gather.14 = f32[64,256]{1,0:T(8,128)S(1)} all-gather(f32[16,256]{1,0:T(8,128)} %param.11), channel_id=1, replica_groups=mesh['batch'=4,'centre'=8] {'batch'}, dimensions={0}, use_global_device_ids=true | all-gather | bytes 81920 | tf_op jit(solution)/shard_map/all_gather | solution.py:22
  17.2 0.0 copy-done.4
  17.2 8.8 %all_gather.13 = f32[64,1024]{1,0:T(8,128)S(1)} all-gather(f32[16,1024]{1,0:T(8,128)S(1)} %copy-done.4), channel_id=1, replica_groups=mesh['batch'=4,'centre'=8] {'batch'}, dimensions={0}, use_global_device_ids=true | all-gather | bytes 327680 | tf_op jit(solution)/shard_map/all_gather | solution.py:21
  26.0 0.0 copy-done
  26.0 0.6 gather_fusion
  26.6 0.1 broadcast_select_fusion
  26.7 15.2 %all_gather.12 = f32[128,1024]{1,0:T(8,128)S(1)} all-gather(f32[128,128]{1,0:T(8,128)S(1)} %broadcast_select_fusion), channel_id=1, replica_groups=mesh['batch'=4,'centre'=8] {'centre'}, dimensions={1}, use_global_device_ids=true | all-gather | bytes 589824 | tf_op jit(solution)/shard_map/all_gather | solution.py:10
  41.9 0.7 fusion
  42.6 1.1 convolution_bitcast_fusion.1
  43.7 0.0 copy-start.5
  43.7 0.0 reduce-scatter.7.cloned.1.call-update
  43.7 0.0 reduce-scatter.5.cloned.1.call-start
  43.7 0.8 copy-done.5
  44.6 0.1 constant_dynamic-slice_fusion
  44.6 0.1 copy.15
  44.7 29.7 %reduce-scatter.7.cloned.1.call-done = f32[32,128]{1,0:T(8,128)} async-done(((f32[256,128]{1,0:T(8,128)}), f32[32,128]{1,0:T(8,128)}) %reduce-scatter.7.cloned.1.call-update) | async-done | bytes 16400
  74.4 0.7 fusion.6
  75.1 13.9 %all_gather.15 = f32[128,256]{0,1:T(8,128)S(1)} all-gather(f32[128,32]{0,1:T(8,128)S(1)} %fusion.6), channel_id=1, replica_groups=mesh['batch'=4,'centre'=8] {'centre'}, dimensions={1}, use_global_device_ids=true | all-gather | bytes 147456 | tf_op jit(solution)/shard_map/all_gather | solution.py:39
  89.0 0.9 fusion.10
  89.9 0.0 copy-start.1
  89.9 0.0 reduce-scatter.5.cloned.1.call-update
  90.0 0.0 all-reduce.2.cloned.1.call-start
  90.0 22.3 %reduce-scatter.5.cloned.1.call-done = f32[16,256]{1,0:T(8,128)} async-done(((f32[64,256]{1,0:T(8,128)}), f32[16,256]{1,0:T(8,128)}) %reduce-scatter.5.cloned.1.call-update) | async-done | bytes 16400 | tf_op jit(solution)/shard_map/reduce_scatter | solution.py:41
  112.3 0.0 copy-done.1
  112.3 2.8 %convolution_bitcast_fusion = f32[1024,256]{0,1:T(8,128)} fusion(f32[16,1024]{1,0:T(8,128)S(1)} %copy-done.1, f32[16,256]{1,0:T(8,128)} %reduce-scatter.5.cloned.1.call-done), kind=kOutput, calls=%fused_computation.1 | convolution fusion | flops 50335744 | bytes 1130496 | tf_op jit(solution)/shard_map/dot_general | solution.py:55
  115.1 0.0 copy-start.2
  115.1 0.0 copy-start.3
  115.1 0.0 copy-start.6
  115.1 0.0 all-reduce.2.cloned.1.call-update
  115.1 133.1 %all-reduce.2.cloned.1.call-done = f32[1024,256]{0,1:T(8,128)} async-done(((f32[1024,256]{0,1:T(8,128)}), f32[1024,256]{0,1:T(8,128)}) %all-reduce.2.cloned.1.call-update) | async-done | bytes 1048592 | tf_op jit(solution)/shard_map/psum | solution.py:62
  248.2 0.0 copy-done.2
  248.2 0.0 copy-done.3
  248.2 0.0 copy-done.6
  248.2 2.8 %fusion.3 = f32[16,256]{1,0:T(8,128)} fusion(f32[16,256]{1,0:T(8,128)S(1)} %copy-done.3, f32[16,1024]{1,0:T(8,128)S(1)} %copy-done.1, f32[1024,256]{0,1:T(8,128)} %all-reduce.2.cloned.1.call-done, f32[1024]{0:T(1024)S(1)} %copy-done.6, f32[16,256]{1,0:T(8,128)S(1)} %copy-done.2), kind=kOutput, calls=%fused_computation.8 | convolution fusion | flops 50610176 | bytes 1167360 | tf_op jit(solution)/shard_map/dot_general | solution.py:63
  (2 shorter events, 0.0 us)
Async XLA Ops:
  6.5 19.4 %copy-start = (f32[256,128]{1,0:T(8,128)S(1)}, f32[256,128]{1,0:T(8,128)}, u32[]{:S(2)}) copy-start(f32[256,128]{1,0:T(8,128)} %param.7) | copy-start | bytes 393220
  6.5 0.7 copy-start.7
  6.5 10.6 %copy-start.4 = (f32[16,1024]{1,0:T(8,128)S(1)}, f32[16,1024]{1,0:T(8,128)}, u32[]{:S(2)}) copy-start(f32[16,1024]{1,0:T(8,128)} %param.10) | copy-start | bytes 196612
  6.5 67.8 %reduce-scatter.7.cloned.1.call-start = ((), (), s32[]{:S(2)}) async-start(), calls=%async_computation.4 | async-start | bytes 147456
  43.7 0.9 copy-start.5
  43.7 68.7 %reduce-scatter.5.cloned.1.call-start = ((), (), s32[]{:S(2)}) async-start(), calls=%async_computation.2 | async-start | bytes 81920 | tf_op jit(solution)/shard_map/reduce_scatter | solution.py:41
  89.9 22.4 %copy-start.1 = (f32[16,1024]{1,0:T(8,128)S(1)}, f32[16,1024]{1,0:T(8,128)}, u32[]{:S(2)}) copy-start(f32[16,1024]{1,0:T(8,128)} %param.12) | copy-start | bytes 196612
  90.0 158.2 %all-reduce.2.cloned.1.call-start = ((), (), s32[]{:S(2)}) async-start(), calls=%async_computation.3 | async-start | bytes 2097152 | tf_op jit(solution)/shard_map/psum | solution.py:62
  115.1 133.1 %copy-start.2 = (f32[16,256]{1,0:T(8,128)S(1)}, f32[16,256]{1,0:T(8,128)}, u32[]{:S(2)}) copy-start(f32[16,256]{1,0:T(8,128)} %reduce-scatter.5.cloned.1.call-done) | copy-start | bytes 49156
  115.1 133.1 %copy-start.3 = (f32[16,256]{1,0:T(8,128)S(1)}, f32[16,256]{1,0:T(8,128)}, u32[]{:S(2)}) copy-start(f32[16,256]{1,0:T(8,128)} %param.11) | copy-start | bytes 49156
  115.1 133.1 %copy-start.6 = (f32[1024]{0:T(1024)S(1)}, f32[1024]{0:T(1024)}, u32[]{:S(2)}) copy-start(f32[1024]{0:T(1024)} %param.13) | copy-start | bytes 12292
Sparse Core Ops, SparseCore 0:
  43.8 30.5 reduce-scatter.6
  90.1 22.1 reduce-scatter.4
  117.5 130.6 all-reduce.1
where the time goes:
time: 258 us
  waiting for transfers between devices  185 us (72%)
  blocking collectives  47.8 us (19%)
  between operations  13.2 us (5%)
  matrix products  8.16 us (3%)
    psum x1, waiting for transfers between devices, on_device(): coords = lax.psum(local_coords, ('batch', 'centre'))  133 us
    unnamed x4, waiting for transfers between devices  29.7 us
    reduce_scatter x1, waiting for transfers between devices, on_device(): lax.psum_scatter(lax.dot_general(kernel, residual, (((0,), (0,)), ((), ()...  22.3 us
    all_gather x1, blocking collectives, on_device(): batch_x = lax.all_gather(picked, 'centre', axis=1, tiled=True)  15.2 us
    all_gather x1, blocking collectives, on_device(): lax.all_gather(columns - own_targets, 'centre', axis=1, tiled=True)  13.9 us
    all_gather x1, blocking collectives, on_device(): crows = lax.all_gather(coeffs, 'batch', axis=0, tiled=True)  9.88 us
    all_gather x1, blocking collectives, on_device(): zrows = lax.all_gather(centres, 'batch', axis=0, tiled=True)  8.8 us
  transfers between devices with their start and end apart: 3, of which 3 were waited for; matrix products, arithmetic and copies ran while one was open for 0% of the time, Pallas kernels for 0%

commit v1 on v0

v1 whole, which is shorter than its diff:
```python
import jax
import jax.numpy as jnp
from jax import lax
from jax.experimental import pallas as pl
from jax.experimental.pallas import tpu as pltpu
from jax.sharding import PartitionSpec as P

MESH = pl.DeviceIdType.MESH
F32 = jnp.float32


def mm(a, b, dims):
    return lax.dot_general(
        a, b, (dims, ((), ())), precision=lax.Precision.HIGHEST, preferred_element_type=F32
    )


def rows_of(buf):
    count, depth, width = buf.shape
    if depth % 8 == 0:
        return buf[...].reshape(count * depth, width)
    return jnp.concatenate([buf[j] for j in range(count)], axis=0)


def step_kernel(
    nb, nc, inv_width, model_norm, step_size,
    x_ref, t_ref, z_ref, a_ref, e_ref, s_ref, out_ref,
    xs, ec, zs, cs, eb, pout, pin, rs, gs, gsum, cout, cin,
    x_send, x_recv, ec_send, ec_recv, b_send, b_recv,
    p_send, p_recv, r_send, r_recv, g_send, g_recv, c_send, c_recv,
):
    b = lax.axis_index("batch")
    c = lax.axis_index("centre")
    own = z_ref.shape[0]
    part = t_ref.shape[1]
    width = x_ref.shape[1]
    mate = c + 1 - 2 * lax.rem(c, 2)
    others = [lax.rem(c + k, nc) for k in range(1, nc)]
    groups = [lax.rem(b + k, nb) for k in range(1, nb)]
    pending = []

    def push(src, dst, send, recv, bi, ci):
        copy = pltpu.make_async_remote_copy(
            src_ref=src, dst_ref=dst, send_sem=send, recv_sem=recv,
            device_id=(bi, ci), device_id_type=MESH,
        )
        copy.start()
        pending.append(copy)

    def arrived(dst, recv):
        pltpu.make_async_remote_copy(
            src_ref=dst, dst_ref=dst, send_sem=recv, recv_sem=recv,
            device_id=(b, mate), device_id_type=MESH,
        ).wait_recv()

    barrier = pltpu.get_barrier_semaphore()
    for ci in others:
        pl.semaphore_signal(barrier, inc=1, device_id=(b, ci), device_id_type=MESH)
    for bi in groups:
        pl.semaphore_signal(barrier, inc=1, device_id=(bi, c), device_id_type=MESH)
    pl.semaphore_wait(barrier, nc - 1 + nb - 1)

    half = nc // 2
    peers = [lax.rem(c + 2 * k, nc) for k in range(1, half)]
    for k, ci in enumerate(peers):
        push(x_ref, xs.at[c], x_send.at[k], x_recv.at[c], b, ci)
    push(x_ref, xs.at[c], x_send.at[half - 1], x_recv.at[c], b, mate)
    for k, bi in enumerate(groups):
        push(z_ref, zs.at[b], b_send.at[0, k], b_recv.at[0, b], bi, c)
    for k, bi in enumerate(groups):
        push(a_ref, cs.at[b], b_send.at[1, k], b_recv.at[1, b], bi, c)
    for k, ci in enumerate(peers):
        push(e_ref, ec.at[c], ec_send.at[k], ec_recv.at[c], b, ci)
    push(e_ref, ec.at[c], ec_send.at[half - 1], ec_recv.at[c], b, mate)
    for k, bi in enumerate(groups):
        push(e_ref, eb.at[b], b_send.at[2, k], b_recv.at[2, b], bi, c)
    xs[c] = x_ref[...]
    ec[c] = e_ref[...]
    zs[b] = z_ref[...]
    cs[b] = a_ref[...]
    eb[b] = e_ref[...]

    sources = [lax.rem(c + nc - 2 * k, nc) for k in range(1, half)]
    for k, ci in enumerate(sources):
        arrived(xs.at[ci], x_recv.at[ci])
        push(xs.at[ci], xs.at[ci], x_send.at[half + k], x_recv.at[ci], b, mate)
    for bi in groups:
        arrived(zs.at[bi], b_recv.at[0, bi])
    arrived(xs.at[mate], x_recv.at[mate])
    for k in range(1, half):
        ci = lax.rem(mate + nc - 2 * k, nc)
        arrived(xs.at[ci], x_recv.at[ci])

    scores = None
    for j in range(nc):
        zj = zs[:, :, j * width:(j + 1) * width].reshape(nb * own, width)
        term = mm(xs[j], zj, ((1,), (1,)))
        scores = term if scores is None else scores + term
    kernel = jnp.exp(scores * inv_width)
    for bi in groups:
        arrived(cs.at[bi], b_recv.at[1, bi])
    value = mm(kernel, rows_of(cs), ((1,), (0,)))
    for j in range(nc):
        pout[j] = value[j * part:(j + 1) * part]
    for k, ci in enumerate(others):
        push(pout.at[ci], pin.at[c], p_send.at[k], p_recv.at[c], b, ci)
    pin[c] = pout[c]

    for k, ci in enumerate(sources):
        arrived(ec.at[ci], ec_recv.at[ci])
        push(ec.at[ci], ec.at[ci], ec_send.at[half + k], ec_recv.at[ci], b, mate)

    for ci in others:
        arrived(pin.at[ci], p_recv.at[ci])
    total = pin[0]
    for j in range(1, nc):
        total = total + pin[j]
    rs[c] = total * model_norm - t_ref[c]
    for k, ci in enumerate(others):
        push(rs.at[c], rs.at[c], r_send.at[k], r_recv.at[c], b, ci)

    arrived(ec.at[mate], ec_recv.at[mate])
    for k in range(1, half):
        ci = lax.rem(mate + nc - 2 * k, nc)
        arrived(ec.at[ci], ec_recv.at[ci])
    for bi in groups:
        arrived(eb.at[bi], b_recv.at[2, bi])
    mix = mm(rows_of(ec) * s_ref[...], rows_of(eb), ((1,), (1,)))
    kernel_t = kernel.T

    for ci in others:
        arrived(rs.at[ci], r_recv.at[ci])
    gs[b] = mm(kernel_t, rows_of(rs), ((1,), (0,)))
    for k, bi in enumerate(groups):
        push(gs.at[b], gs.at[b], g_send.at[k], g_recv.at[b], bi, c)
    for bi in groups:
        arrived(gs.at[bi], g_recv.at[bi])
    grad = gs[0]
    for j in range(1, nb):
        grad = grad + gs[j]
    grad = grad * model_norm
    gsum[...] = grad.reshape(nb, own, grad.shape[1])
    moved = mm(mix, grad, ((1,), (0,)))
    for j in range(nc):
        cout[j] = moved[j * own:(j + 1) * own]
    for k, ci in enumerate(others):
        push(cout.at[ci], cin.at[c], c_send.at[k], c_recv.at[c], b, ci)
    cin[c] = cout[c]
    for ci in others:
        arrived(cin.at[ci], c_recv.at[ci])
    fix = cin[0]
    for j in range(1, nc):
        fix = fix + cin[j]
    out_ref[...] = a_ref[...] - step_size * (gsum[b] - fix)
    for copy in pending:
        copy.wait_send()


def on_device(pool, sample_index, targets, centres, coeffs, eigvecs, eigscale):
    nb = lax.axis_size("batch")
    nc = lax.axis_size("centre")
    picked = jnp.take(pool, sample_index, axis=0)
    rows, part_width = picked.shape
    own, features = centres.shape
    outputs = targets.shape[1]
    eigen = eigvecs.shape[1]
    total_centres = own * nb * nc
    part = rows // nc
    body = lambda *refs: step_kernel(
        nb, nc, features ** -0.5, total_centres ** -0.5,
        0.5 * (total_centres / (rows * nb)) ** 0.5, *refs
    )
    dma = pltpu.SemaphoreType.DMA
    vmem = lambda *dims: pltpu.VMEM(dims, F32)
    return pl.pallas_call(
        body,
        out_shape=jax.ShapeDtypeStruct((own, outputs), F32),
        in_specs=[pl.BlockSpec(memory_space=pltpu.VMEM)] * 6,
        out_specs=pl.BlockSpec(memory_space=pltpu.VMEM),
        scratch_shapes=[
            vmem(nc, rows, part_width),
            vmem(nc, own, eigen),
            vmem(nb, own, features),
            vmem(nb, own, outputs),
            vmem(nb, own, eigen),
            vmem(nc, part, outputs),
            vmem(nc, part, outputs),
            vmem(nc, part, outputs),
            vmem(nb, nb * own, outputs),
            vmem(nb, own, outputs),
            vmem(nc, own, outputs),
            vmem(nc, own, outputs),
            dma((nc,)), dma((nc,)),
            dma((nc,)), dma((nc,)),
            dma((3, nb)), dma((3, nb)),
            dma((nc,)), dma((nc,)),
            dma((nc,)), dma((nc,)),
            dma((nb,)), dma((nb,)),
            dma((nc,)), dma((nc,)),
        ],
        compiler_params=pltpu.CompilerParams(
            collective_id=0, has_side_effects=True, vmem_limit_bytes=48 * 1024 * 1024
        ),
    )(
        picked,
        targets.reshape(nc, part, outputs),
        centres,
        coeffs,
        eigvecs,
        eigscale[None, :],
    )


def solution(mesh):
    return jax.shard_map(
        on_device,
        mesh=mesh,
        in_specs=(
            P("batch", "centre"),
            P("batch"),
            P("batch", None),
            P(("batch", "centre"), None),
            P(("batch", "centre"), None),
            P(("batch", "centre"), None),
            P(),
        ),
        out_specs=P(("batch", "centre"), None),
        check_vma=False,
    )
```

time: 258 us -> 39 us (0.15)
  waiting for transfers between devices: 185 us -> 0 us
  blocking collectives: 47.8 us -> 0 us
  Pallas kernels: 0 us -> 35.7 us
  between operations: 13.2 us -> 0.04 us
  matrix products: 8.16 us -> 0 us
    psum x1 -> x0, waiting for transfers between devices: 133 us -> none  [on_device(): coords = lax.psum(local_coords, ('batch', 'centre'))]
    all_gather x4 -> x0, blocking collectives: 47.8 us -> none  [the longest x1 15.2 us: on_device(): batch_x = lax.all_gather(picked, 'centre', axis=1, tiled=True)]
    pallas_call x0 -> x1, Pallas kernels: none -> 35.7 us  [on_device(): pl.pallas_call(body, out_shape=jax.ShapeDtypeStruct((own, outputs), F32),...]
    unnamed x4 -> x0, waiting for transfers between devices: 29.7 us -> none
    reduce_scatter x1 -> x0, waiting for transfers between devices: 22.3 us -> none  [on_device(): lax.psum_scatter(lax.dot_general(kernel, residual, (((0,), (0,)), ((), ()...]
    dot_general x4 -> x0, matrix products: 7.11 us -> none  [the longest x1 2.77 us: on_device(): lax.dot_general(eigvecs, gradient, (((0,), (0,)), ((), ())), precision=hi...]
  transfers between devices with their start and end apart: 3 -> 0, of which waited for: 3 -> 0; matrix products, arithmetic and copies ran while one was open for 0% -> 0% of each run, Pallas kernels for 0% -> 0%
where the time goes in v1:
time: 39 us; the launch traced here: 38.8 us
  Pallas kernels  35.7 us (92%)
  local copies, waits for them, and re-layouts  2.98 us (8%)
    pallas_call x1, Pallas kernels, on_device(): pl.pallas_call(body, out_shape=jax.ShapeDtypeStruct((own, outputs), F32),...  35.7 us
    unnamed x15, local copies, waits for them, and re-layouts  2.33 us

profile of v1, /device:TPU:0, one launch (start us, length us, event | category | flops | bytes accessed | tf_op | source)
XLA Modules:
  0.0 38.8 jit_solution(326019634856041107)
XLA Ops:
  0.0 0.0 copy-start
  0.0 0.0 copy-start.6
  0.0 0.7 %copy-done.6 = s32[128]{0:T(128)S(1)} copy-done((s32[128]{0:T(128)S(1)}, s32[128]{0:T(128)}, u32[]{:S(2)}) %copy-start.6) | copy-done | bytes 536
  0.7 0.2 copy-done
  0.9 0.0 copy-start.2
  0.9 0.0 copy-start.3
  0.9 0.0 copy-start.4
  0.9 0.0 copy-start.5
  0.9 0.6 %gather_fusion = f32[128,128]{1,0:T(8,128)S(1)} fusion(f32[256,128]{1,0:T(8,128)S(1)} %copy-done, s32[1024]{0:T(1024)S(1)} %pad_clamp_fusion), kind=kCustom, calls=%fused_computation | custom fusion | bytes 131584 | tf_op jit(solution)/shard_map/jit(_take)/gather | solution.py:162
  1.6 0.0 copy-start.1
  1.6 0.1 broadcast_select_fusion.refs_0_
  1.7 0.1 copy-done.2
  1.8 0.0 copy-done.3
  1.8 0.0 copy-done.4
  1.8 0.0 copy-done.5
  1.8 0.7 %copy-done.1 = f32[128,256]{1,0:T(8,128)S(1)} copy-done((f32[128,256]{1,0:T(8,128)S(1)}, f32[128,256]{1,0:T(8,128)}, u32[]{:S(2)}) %copy-start.1) | copy-done | bytes 131096
  2.5 35.7 %shard_map.73 = f32[16,256]{1,0:T(8,128)S(1)} custom-call(f32[128,128]{1,0:T(8,128)S(1)} %broadcast_select_fusion.refs_0_, f32[8,16,256]{2,1,0:T(8,128)S(1)} %bitcast.2, f32[16,1024]{1,0:T(8,128)S(1)} %copy-done.2, f32[16,256]{1,0:T(8,128)S(1)} %copy-done.4, f32[16,1024]{1,0:T(8,128)S(1)} %copy-done.3, f32[1,1024]{1,0:T(1,128)S(1)} %bitcast.3), custom_call_target="tpu_custom_call" | custom-call | tf_op jit(solution)/shard_map/pallas_call | solution.py:175
  38.2 0.6 %copy.9 = f32[16,256]{1,0:T(8,128)} copy(f32[16,256]{1,0:T(8,128)S(1)} %shard_map.73) | data formatting | bytes 32768
  (3 shorter events, 0.0 us)
Async XLA Ops:
  0.0 0.9 %copy-start = (f32[256,128]{1,0:T(8,128)S(1)}, f32[256,128]{1,0:T(8,128)}, u32[]{:S(2)}) copy-start(f32[256,128]{1,0:T(8,128)} %param.7) | copy-start | bytes 393220
  0.0 0.7 %copy-start.6 = (s32[128]{0:T(128)S(1)}, s32[128]{0:T(128)}, u32[]{:S(2)}) copy-start(s32[128]{0:T(128)} %param.8) | copy-start | bytes 1540
  0.9 0.8 %copy-start.2 = (f32[16,1024]{1,0:T(8,128)S(1)}, f32[16,1024]{1,0:T(8,128)}, u32[]{:S(2)}) copy-start(f32[16,1024]{1,0:T(8,128)} %refs_2_.1) | copy-start | bytes 196612
  0.9 0.9 %copy-start.3 = (f32[16,1024]{1,0:T(8,128)S(1)}, f32[16,1024]{1,0:T(8,128)}, u32[]{:S(2)}) copy-start(f32[16,1024]{1,0:T(8,128)} %refs_4_.1) | copy-start | bytes 196612
  0.9 0.9 %copy-start.4 = (f32[16,256]{1,0:T(8,128)S(1)}, f32[16,256]{1,0:T(8,128)}, u32[]{:S(2)}) copy-start(f32[16,256]{1,0:T(8,128)} %refs_3_.1) | copy-start | bytes 49156
  0.9 0.9 %copy-start.5 = (f32[1024]{0:T(1024)S(1)}, f32[1024]{0:T(1024)}, u32[]{:S(2)}) copy-start(f32[1024]{0:T(1024)} %param.13) | copy-start | bytes 12292
  1.6 0.9 %copy-start.1 = (f32[128,256]{1,0:T(8,128)S(1)}, f32[128,256]{1,0:T(8,128)}, u32[]{:S(2)}) copy-start(f32[128,256]{1,0:T(8,128)} %param.9) | copy-start | bytes 393220

commit v2 on v1

--- a/solution.py
+++ b/solution.py
@@ -24,16 +24,16 @@
 
 def step_kernel(
     nb, nc, inv_width, model_norm, step_size,
-    x_ref, t_ref, z_ref, a_ref, e_ref, s_ref, out_ref,
-    xs, ec, zs, cs, eb, pout, pin, rs, gs, gsum, cout, cin,
+    pool_hbm, i_hbm, t_hbm, z_hbm, a_hbm, e_hbm, s_hbm, out_ref,
+    pool_ref, i_ref, t_ref, s_ref, zcol, local, xs, ec, zs, cs, eb, pout, pin, rs, gs, gsum, cout, cin,
     x_send, x_recv, ec_send, ec_recv, b_send, b_recv,
     p_send, p_recv, r_send, r_recv, g_send, g_recv, c_send, c_recv,
 ):
     b = lax.axis_index("batch")
     c = lax.axis_index("centre")
-    own = z_ref.shape[0]
-    part = t_ref.shape[1]
-    width = x_ref.shape[1]
+    own = z_hbm.shape[0]
+    part = t_hbm.shape[1]
+    width = pool_hbm.shape[1]
     mate = c + 1 - 2 * lax.rem(c, 2)
     others = [lax.rem(c + k, nc) for k in range(1, nc)]
     groups = [lax.rem(b + k, nb) for k in range(1, nb)]
@@ -58,44 +58,55 @@
         pl.semaphore_signal(barrier, inc=1, device_id=(b, ci), device_id_type=MESH)
     for bi in groups:
         pl.semaphore_signal(barrier, inc=1, device_id=(bi, c), device_id_type=MESH)
+    fetches = []
+    for k, (src, dst) in enumerate([
+        (pool_hbm, pool_ref), (i_hbm, i_ref), (z_hbm, zs.at[b]), (a_hbm, cs.at[b]),
+        (e_hbm, ec.at[c]), (e_hbm, eb.at[b]), (s_hbm, s_ref), (t_hbm.at[c], t_ref),
+    ]):
+        copy = pltpu.make_async_copy(src, dst, local.at[k])
+        copy.start()
+        fetches.append(copy)
+    fetches[0].wait()
+    fetches[1].wait()
+    rows = i_ref.shape[1]
+    lines = lax.broadcasted_iota(jnp.int32, (pool_ref.shape[0], rows), 0)
+    chosen = jnp.where(lines == i_ref[...], 1.0, 0.0).astype(F32)
+    xs[c] = mm(chosen, pool_ref[...], ((0,), (0,)))
+    for copy in fetches[2:]:
+        copy.wait()
     pl.semaphore_wait(barrier, nc - 1 + nb - 1)
 
     half = nc // 2
     peers = [lax.rem(c + 2 * k, nc) for k in range(1, half)]
     for k, ci in enumerate(peers):
-        push(x_ref, xs.at[c], x_send.at[k], x_recv.at[c], b, ci)
-    push(x_ref, xs.at[c], x_send.at[half - 1], x_recv.at[c], b, mate)
-    for k, bi in enumerate(groups):
-        push(z_ref, zs.at[b], b_send.at[0, k], b_recv.at[0, b], bi, c)
-    for k, bi in enumerate(groups):
-        push(a_ref, cs.at[b], b_send.at[1, k], b_recv.at[1, b], bi, c)
+        push(xs.at[c], xs.at[c], x_send.at[k], x_recv.at[c], b, ci)
+    push(xs.at[c], xs.at[c], x_send.at[half - 1], x_recv.at[c], b, mate)
+    for k, bi in enumerate(groups):
+        push(zs.at[b], zs.at[b], b_send.at[0, k], b_recv.at[0, b], bi, c)
+    for k, bi in enumerate(groups):
+        push(cs.at[b], cs.at[b], b_send.at[1, k], b_recv.at[1, b], bi, c)
     for k, ci in enumerate(peers):
-        push(e_ref, ec.at[c], ec_send.at[k], ec_recv.at[c], b, ci)
-    push(e_ref, ec.at[c], ec_send.at[half - 1], ec_recv.at[c], b, mate)
-    for k, bi in enumerate(groups):
-        push(e_ref, eb.at[b], b_send.at[2, k], b_recv.at[2, b], bi, c)
-    xs[c] = x_ref[...]
-    ec[c] = e_ref[...]
-    zs[b] = z_ref[...]
-    cs[b] = a_ref[...]
-    eb[b] = e_ref[...]
+        push(ec.at[c], ec.at[c], ec_send.at[k], ec_recv.at[c], b, ci)
+    push(ec.at[c], ec.at[c], ec_send.at[half - 1], ec_recv.at[c], b, mate)
+    for k, bi in enumerate(groups):
+        push(eb.at[b], eb.at[b], b_send.at[2, k], b_recv.at[2, b], bi, c)
 
     sources = [lax.rem(c + nc - 2 * k, nc) for k in range(1, half)]
+    for bi in groups:
+        arrived(zs.at[bi], b_recv.at[0, bi])
+    for j in range(nc):
+        zcol[j] = zs[:, :, j * width:(j + 1) * width].reshape(nb * own, width)
+    scores = mm(xs[c], zcol[c], ((1,), (1,)))
+    arrived(xs.at[mate], x_recv.at[mate])
+    scores = scores + mm(xs[mate], zcol[mate], ((1,), (1,)))
     for k, ci in enumerate(sources):
         arrived(xs.at[ci], x_recv.at[ci])
         push(xs.at[ci], xs.at[ci], x_send.at[half + k], x_recv.at[ci], b, mate)
-    for bi in groups:
-        arrived(zs.at[bi], b_recv.at[0, bi])
-    arrived(xs.at[mate], x_recv.at[mate])
+        scores = scores + mm(xs[ci], zcol[ci], ((1,), (1,)))
     for k in range(1, half):
         ci = lax.rem(mate + nc - 2 * k, nc)
         arrived(xs.at[ci], x_recv.at[ci])
-
-    scores = None
-    for j in range(nc):
-        zj = zs[:, :, j * width:(j + 1) * width].reshape(nb * own, width)
-        term = mm(xs[j], zj, ((1,), (1,)))
-        scores = term if scores is None else scores + term
+        scores = scores + mm(xs[ci], zcol[ci], ((1,), (1,)))
     kernel = jnp.exp(scores * inv_width)
     for bi in groups:
         arrived(cs.at[bi], b_recv.at[1, bi])
@@ -115,7 +126,7 @@
     total = pin[0]
     for j in range(1, nc):
         total = total + pin[j]
-    rs[c] = total * model_norm - t_ref[c]
+    rs[c] = total * model_norm - t_ref[...]
     for k, ci in enumerate(others):
         push(rs.at[c], rs.at[c], r_send.at[k], r_recv.at[c], b, ci)
 
@@ -151,7 +162,7 @@
     fix = cin[0]
     for j in range(1, nc):
         fix = fix + cin[j]
-    out_ref[...] = a_ref[...] - step_size * (gsum[b] - fix)
+    out_ref[...] = cs[b] - step_size * (gsum[b] - fix)
     for copy in pending:
         copy.wait_send()
 
@@ -159,8 +170,8 @@
 def on_device(pool, sample_index, targets, centres, coeffs, eigvecs, eigscale):
     nb = lax.axis_size("batch")
     nc = lax.axis_size("centre")
-    picked = jnp.take(pool, sample_index, axis=0)
-    rows, part_width = picked.shape
+    rows = sample_index.shape[0]
+    part_width = pool.shape[1]
     own, features = centres.shape
     outputs = targets.shape[1]
     eigen = eigvecs.shape[1]
@@ -175,9 +186,15 @@
     return pl.pallas_call(
         body,
         out_shape=jax.ShapeDtypeStruct((own, outputs), F32),
-        in_specs=[pl.BlockSpec(memory_space=pltpu.VMEM)] * 6,
+        in_specs=[pl.BlockSpec(memory_space=pltpu.HBM)] * 7,
         out_specs=pl.BlockSpec(memory_space=pltpu.VMEM),
         scratch_shapes=[
+            vmem(*pool.shape),
+            pltpu.VMEM((1, rows), jnp.int32),
+            vmem(part, outputs),
+            vmem(1, eigen),
+            vmem(nc, nb * own, part_width),
+            dma((8,)),
             vmem(nc, rows, part_width),
             vmem(nc, own, eigen),
             vmem(nb, own, features),
@@ -199,10 +216,11 @@
             dma((nc,)), dma((nc,)),
         ],
         compiler_params=pltpu.CompilerParams(
-            collective_id=0, has_side_effects=True, vmem_limit_bytes=48 * 1024 * 1024
+            collective_id=0, has_side_effects=True, vmem_limit_bytes=67043328
         ),
     )(
-        picked,
+        pool,
+        sample_index[None, :],
         targets.reshape(nc, part, outputs),
         centres,
         coeffs,

time: 39 us -> 37.9 us (0.972)
  local copies, waits for them, and re-layouts: 2.98 us -> 1.32 us
  Pallas kernels: 35.7 us -> 36.3 us
    unnamed x15 -> x1, local copies, waits for them, and re-layouts: 2.33 us -> 1.32 us
    gather x1 -> x0, local copies, waits for them, and re-layouts: 0.65 us -> none  [on_device(): picked = jnp.take(pool, sample_index, axis=0)]
    pallas_call x1, Pallas kernels: 35.7 us -> 36.3 us  [on_device(): pl.pallas_call(body, out_shape=jax.ShapeDtypeStruct((own, outputs), F32),...]
where the time goes in v2:
time: 37.9 us; the launch traced here: 37.7 us
  Pallas kernels  36.3 us (96%)
  local copies, waits for them, and re-layouts  1.32 us (3%)
    pallas_call x1, Pallas kernels, on_device(): pl.pallas_call(body, out_shape=jax.ShapeDtypeStruct((own, outputs), F32),...  36.3 us
    unnamed x1, local copies, waits for them, and re-layouts  1.32 us

profile of v2, /device:TPU:0, one launch (start us, length us, event | category | flops | bytes accessed | tf_op | source)
XLA Modules:
  0.0 37.7 jit_solution(8340027515455258135)
XLA Ops:
  0.0 36.3 %shard_map.73 = f32[16,256]{1,0:T(8,128)} custom-call(f32[256,128]{1,0:T(8,128)} %refs_0_.1, s32[1,128]{1,0:T(1,128)} %bitcast.5, f32[8,16,256]{2,1,0:T(8,128)} %bitcast.3, f32[16,1024]{1,0:T(8,128)} %refs_3_.1, f32[16,256]{1,0:T(8,128)} %refs_4_.1, f32[16,1024]{1,0:T(8,128)} %refs_5_.1, f32[1,1024]{1,0:T(1,128)} %bitcast.4), custom_call_target="tpu_custom_call" | custom-call | tf_op jit(solution)/shard_map/pallas_call | solution.py:186
  36.4 1.3 %copy.9 = f32[16,256]{1,0:T(8,128)} copy(f32[16,256]{1,0:T(8,128)} %shard_map.73) | data formatting | bytes 32768

commit v3 on v2

--- a/solution.py
+++ b/solution.py
@@ -15,6 +15,17 @@
     )
 
 
+def halves(a):
+    high = a.astype(jnp.bfloat16)
+    return high, (a - high.astype(F32)).astype(jnp.bfloat16)
+
+
+def mm3(left, right):
+    dot = lambda a, b: jnp.dot(a, b, preferred_element_type=F32)
+    (ah, al), (bh, bl) = left, right
+    return dot(ah, bh) + (dot(ah, bl) + dot(al, bh))
+
+
 def rows_of(buf):
     count, depth, width = buf.shape
     if depth % 8 == 0:
@@ -23,7 +34,7 @@
 
 
 def step_kernel(
-    nb, nc, inv_width, model_norm, step_size,
+    nb, nc, inv_width, model_norm,
     pool_hbm, i_hbm, t_hbm, z_hbm, a_hbm, e_hbm, s_hbm, out_ref,
     pool_ref, i_ref, t_ref, s_ref, zcol, local, xs, ec, zs, cs, eb, pout, pin, rs, gs, gsum, cout, cin,
     x_send, x_recv, ec_send, ec_recv, b_send, b_recv,
@@ -96,6 +107,9 @@
         arrived(zs.at[bi], b_recv.at[0, bi])
     for j in range(nc):
         zcol[j] = zs[:, :, j * width:(j + 1) * width].reshape(nb * own, width)
+    for bi in groups:
+        arrived(cs.at[bi], b_recv.at[1, bi])
+    weights = halves(rows_of(cs))
     scores = mm(xs[c], zcol[c], ((1,), (1,)))
     arrived(xs.at[mate], x_recv.at[mate])
     scores = scores + mm(xs[mate], zcol[mate], ((1,), (1,)))
@@ -108,9 +122,7 @@
         arrived(xs.at[ci], x_recv.at[ci])
         scores = scores + mm(xs[ci], zcol[ci], ((1,), (1,)))
     kernel = jnp.exp(scores * inv_width)
-    for bi in groups:
-        arrived(cs.at[bi], b_recv.at[1, bi])
-    value = mm(kernel, rows_of(cs), ((1,), (0,)))
+    value = mm3(halves(kernel), weights)
     for j in range(nc):
         pout[j] = value[j * part:(j + 1) * part]
     for k, ci in enumerate(others):
@@ -136,12 +148,12 @@
         arrived(ec.at[ci], ec_recv.at[ci])
     for bi in groups:
         arrived(eb.at[bi], b_recv.at[2, bi])
-    mix = mm(rows_of(ec) * s_ref[...], rows_of(eb), ((1,), (1,)))
-    kernel_t = kernel.T
+    mix = halves(mm(rows_of(ec) * s_ref[...], rows_of(eb), ((1,), (1,))))
+    kernel_t = halves(kernel.T)
 
     for ci in others:
         arrived(rs.at[ci], r_recv.at[ci])
-    gs[b] = mm(kernel_t, rows_of(rs), ((1,), (0,)))
+    gs[b] = mm3(kernel_t, halves(rows_of(rs)))
     for k, bi in enumerate(groups):
         push(gs.at[b], gs.at[b], g_send.at[k], g_recv.at[b], bi, c)
     for bi in groups:
@@ -151,7 +163,7 @@
         grad = grad + gs[j]
     grad = grad * model_norm
     gsum[...] = grad.reshape(nb, own, grad.shape[1])
-    moved = mm(mix, grad, ((1,), (0,)))
+    moved = mm3(mix, halves(grad))
     for j in range(nc):
         cout[j] = moved[j * own:(j + 1) * own]
     for k, ci in enumerate(others):
@@ -162,7 +174,7 @@
     fix = cin[0]
     for j in range(1, nc):
         fix = fix + cin[j]
-    out_ref[...] = cs[b] - step_size * (gsum[b] - fix)
+    out_ref[...] = gsum[b] - fix
     for copy in pending:
         copy.wait_send()
 
@@ -178,12 +190,11 @@
     total_centres = own * nb * nc
     part = rows // nc
     body = lambda *refs: step_kernel(
-        nb, nc, features ** -0.5, total_centres ** -0.5,
-        0.5 * (total_centres / (rows * nb)) ** 0.5, *refs
+        nb, nc, features ** -0.5, total_centres ** -0.5, *refs
     )
     dma = pltpu.SemaphoreType.DMA
     vmem = lambda *dims: pltpu.VMEM(dims, F32)
-    return pl.pallas_call(
+    delta = pl.pallas_call(
         body,
         out_shape=jax.ShapeDtypeStruct((own, outputs), F32),
         in_specs=[pl.BlockSpec(memory_space=pltpu.HBM)] * 7,
@@ -227,6 +238,7 @@
         eigvecs,
         eigscale[None, :],
     )
+    return coeffs - 0.5 * (total_centres / (rows * nb)) ** 0.5 * delta
 
 
 def solution(mesh):

time: 37.9 us -> 38 us (level)
  other arithmetic: 0 us -> 1.35 us
  local copies, waits for them, and re-layouts: 1.32 us -> 0 us
    sub x0 -> x1, other arithmetic: none -> 1.35 us  [on_device(): return coeffs - 0.5 * (total_centres / (rows * nb)) ** 0.5 * delta]
    unnamed x1 -> x0, local copies, waits for them, and re-layouts: 1.32 us -> none
where the time goes in v3:
time: 38 us; the launch traced here: 37.8 us
  Pallas kernels  36.4 us (96%)
  other arithmetic  1.35 us (4%)
    pallas_call x1, Pallas kernels, on_device(): pl.pallas_call(body, out_shape=jax.ShapeDtypeStruct((own, outputs), F32),...  36.4 us
    sub x1, other arithmetic, on_device(): return coeffs - 0.5 * (total_centres / (rows * nb)) ** 0.5 * delta  1.35 us

profile of v3, /device:TPU:0, one launch (start us, length us, event | category | flops | bytes accessed | tf_op | source)
XLA Modules:
  0.0 37.8 jit_solution(819710074223129426)
XLA Ops:
  0.0 36.4 %shard_map.73 = f32[16,256]{1,0:T(8,128)} custom-call(f32[256,128]{1,0:T(8,128)} %refs_0_.1, s32[1,128]{1,0:T(1,128)} %bitcast.5, f32[8,16,256]{2,1,0:T(8,128)} %bitcast.3, f32[16,1024]{1,0:T(8,128)} %refs_3_.1, f32[16,256]{1,0:T(8,128)} %refs_4_.1, f32[16,1024]{1,0:T(8,128)} %refs_5_.1, f32[1,1024]{1,0:T(1,128)} %bitcast.4), custom_call_target="tpu_custom_call" | custom-call | tf_op jit(solution)/shard_map/pallas_call | solution.py:197
  36.4 1.3 %multiply_subtract_fusion = f32[16,256]{1,0:T(8,128)} fusion(f32[16,256]{1,0:T(8,128)} %refs_4_.1, f32[16,256]{1,0:T(8,128)} %shard_map.73), kind=kLoop, calls=%fused_computation | loop fusion | flops 8192 | bytes 49152 | tf_op jit(solution)/shard_map/sub | solution.py:241

commit v4 on v2

--- a/solution.py
+++ b/solution.py
@@ -13,6 +13,29 @@
     return lax.dot_general(
         a, b, (dims, ((), ())), precision=lax.Precision.HIGHEST, preferred_element_type=F32
     )
+
+
+def farthest_first(z, n):
+    side = z // (n // 2)
+    near = z + side * (n - 1 - 2 * z)
+    lone = n - 1 - 2 * near
+    order = []
+    for k in range(n - 1):
+        paired = (k - lone + n) // n
+        step = paired * (k - lone)
+        beyond = near + (1 - 2 * (step % 2)) * (near - step // 2)
+        chip = (1 - paired) * (n - 1 - k) + paired * beyond
+        order.append(chip + side * (n - 1 - 2 * chip))
+    return order
+
+
+def flipped(b, k):
+    bit = 1
+    while bit <= k:
+        if k & bit:
+            b = b + bit * (1 - 2 * ((b // bit) % 2))
+        bit *= 2
+    return b
 
 
 def rows_of(buf):
@@ -35,8 +58,15 @@
     part = t_hbm.shape[1]
     width = pool_hbm.shape[1]
     mate = c + 1 - 2 * lax.rem(c, 2)
-    others = [lax.rem(c + k, nc) for k in range(1, nc)]
-    groups = [lax.rem(b + k, nb) for k in range(1, nb)]
+    core = lax.rem(c, 2)
+    half = nc // 2
+    chips = farthest_first(c // 2, half)
+    peers = [2 * chip + core for chip in chips]
+    others = [2 * chip + side for chip in chips for side in (core, 1 - core)] + [mate]
+    if nb & (nb - 1):
+        groups = [lax.rem(b + k, nb) for k in range(1, nb)]
+    else:
+        groups = [flipped(b, k) for k in range(nb - 1, 0, -1)]
     pending = []
 
     def push(src, dst, send, recv, bi, ci):
@@ -76,8 +106,6 @@
         copy.wait()
     pl.semaphore_wait(barrier, nc - 1 + nb - 1)
 
-    half = nc // 2
-    peers = [lax.rem(c + 2 * k, nc) for k in range(1, half)]
     for k, ci in enumerate(peers):
         push(xs.at[c], xs.at[c], x_send.at[k], x_recv.at[c], b, ci)
     push(xs.at[c], xs.at[c], x_send.at[half - 1], x_recv.at[c], b, mate)
@@ -91,7 +119,6 @@
     for k, bi in enumerate(groups):
         push(eb.at[b], eb.at[b], b_send.at[2, k], b_recv.at[2, b], bi, c)
 
-    sources = [lax.rem(c + nc - 2 * k, nc) for k in range(1, half)]
     for bi in groups:
         arrived(zs.at[bi], b_recv.at[0, bi])
     for j in range(nc):
@@ -99,12 +126,11 @@
     scores = mm(xs[c], zcol[c], ((1,), (1,)))
     arrived(xs.at[mate], x_recv.at[mate])
     scores = scores + mm(xs[mate], zcol[mate], ((1,), (1,)))
-    for k, ci in enumerate(sources):
+    for k, ci in enumerate(peers):
         arrived(xs.at[ci], x_recv.at[ci])
         push(xs.at[ci], xs.at[ci], x_send.at[half + k], x_recv.at[ci], b, mate)
         scores = scores + mm(xs[ci], zcol[ci], ((1,), (1,)))
-    for k in range(1, half):
-        ci = lax.rem(mate + nc - 2 * k, nc)
+    for ci in [2 * chip + 1 - core for chip in chips]:
         arrived(xs.at[ci], x_recv.at[ci])
         scores = scores + mm(xs[ci], zcol[ci], ((1,), (1,)))
     kernel = jnp.exp(scores * inv_width)
@@ -117,7 +143,7 @@
         push(pout.at[ci], pin.at[c], p_send.at[k], p_recv.at[c], b, ci)
     pin[c] = pout[c]
 
-    for k, ci in enumerate(sources):
+    for k, ci in enumerate(peers):
         arrived(ec.at[ci], ec_recv.at[ci])
         push(ec.at[ci], ec.at[ci], ec_send.at[half + k], ec_recv.at[ci], b, mate)
 
@@ -131,8 +157,7 @@
         push(rs.at[c], rs.at[c], r_send.at[k], r_recv.at[c], b, ci)
 
     arrived(ec.at[mate], ec_recv.at[mate])
-    for k in range(1, half):
-        ci = lax.rem(mate + nc - 2 * k, nc)
+    for ci in [2 * chip + 1 - core for chip in chips]:
         arrived(ec.at[ci], ec_recv.at[ci])
     for bi in groups:
         arrived(eb.at[bi], b_recv.at[2, bi])

time: 37.9 us -> 37.9 us (level)
  no operation moved by 1% of the time
where the time goes in v4:
time: 37.9 us; the launch traced here: 37.7 us
  Pallas kernels  36.3 us (96%)
  local copies, waits for them, and re-layouts  1.32 us (3%)
    pallas_call x1, Pallas kernels, on_device(): pl.pallas_call(body, out_shape=jax.ShapeDtypeStruct((own, outputs), F32),...  36.3 us
    unnamed x1, local copies, waits for them, and re-layouts  1.32 us

profile of v4, /device:TPU:0, one launch (start us, length us, event | category | flops | bytes accessed | tf_op | source)
XLA Modules:
  0.0 37.7 jit_solution(2867204140117039960)
XLA Ops:
  0.0 36.3 %shard_map.73 = f32[16,256]{1,0:T(8,128)} custom-call(f32[256,128]{1,0:T(8,128)} %refs_0_.1, s32[1,128]{1,0:T(1,128)} %bitcast.5, f32[8,16,256]{2,1,0:T(8,128)} %bitcast.3, f32[16,1024]{1,0:T(8,128)} %refs_3_.1, f32[16,256]{1,0:T(8,128)} %refs_4_.1, f32[16,1024]{1,0:T(8,128)} %refs_5_.1, f32[1,1024]{1,0:T(1,128)} %bitcast.4), custom_call_target="tpu_custom_call" | custom-call | tf_op jit(solution)/shard_map/pallas_call | solution.py:211
  36.3 1.3 %copy.9 = f32[16,256]{1,0:T(8,128)} copy(f32[16,256]{1,0:T(8,128)} %shard_map.73) | data formatting | bytes 32768
